TPU v7x, 1024 devices: a whole 8x8x8 slice. The times are simulated.
1024 devices in a mesh: dp: 8 (over y), expert: 8 (over z), tensor: 16 (over x, core).
Axes of the slice: x: 8, y: 8, z: 8, core: 2. Of those that a mesh axis runs over, the one named last changes fastest.
Arguments:
- grad_out: bfloat16 [8192, 6144], P(('dp', 'expert'), 'tensor'), may hold values from -0.1875 to 0.1875
- expert_ids: int32 [8192, 2], P(('dp', 'expert')), may hold values from 0 to 7, all different within a row; in each aligned block of 128 rows (0 to 127, 128 to 255, ...) at most 64 rows name the same one
- route_gates: float32 [8192, 2], P(('dp', 'expert')), may hold values from 0.1 to 1
- saved_hidden: bfloat16 [8, 2048, 16384], P('expert', 'dp', 'tensor'), may hold values from -6 to 6
Outputs:
- weight_grad: bfloat16 [8, 16384, 6144], P('expert', 'tensor', 'dp')
Inputs may be any that keep to these rules, and one draw needn't show every extreme that they name: `expert_ids`: each row names 2 different experts. Among the rows of one device no expert is named by more than 64 rows, and every expert is named somewhere.
All inputs are finite; a program needn't handle non-finite values.
Results may differ from a plain program's by a relative error of at most 0.0049.
Values may be sent and summed in bfloat16 or wider, within the bound.
No kernel may reach another device: no remote copies, remote signals or barrier semaphores. Data moves between devices by JAX's collectives and lax.ppermute only.
A program may use at most 32 MiB of HBM per device.

v0:
```python
import jax
import jax.numpy as jnp
from jax import lax
from jax.sharding import PartitionSpec as P

TOP = 2
CAP = 32


def from_everyone(array, axis):
    copies = jnp.broadcast_to(array, (lax.axis_size(axis), *array.shape))
    return lax.all_to_all(copies, axis, split_axis=0, concat_axis=0, tiled=True)


def laid_out(blocks, dim):
    blocks = jnp.moveaxis(blocks, 0, dim)
    dims = blocks.shape
    return blocks.reshape(*dims[:dim], dims[dim] * dims[dim + 1], *dims[dim + 2 :])


def gathered_copies(array, axis, dim):
    blocks = from_everyone(array, axis)
    return laid_out(blocks, dim)


def slot_table(expert_ids, route_gates, expert_count):
    routes = expert_ids.reshape(-1)
    weights = route_gates.reshape(-1)
    onehot = (routes[:, None] == jnp.arange(expert_count, dtype=jnp.int32)[None, :]).astype(
        jnp.int32
    )
    before = jnp.cumsum(onehot, axis=0) - onehot
    rank = jnp.sum(before * onehot, axis=1)
    target = jnp.where(rank < CAP, routes * CAP + rank, -1)
    match = jnp.arange(expert_count * CAP, dtype=jnp.int32)[:, None] == target[None, :]
    chosen = match.reshape(expert_count * CAP, -1, TOP).any(axis=2)
    slot_gate = jnp.sum(
        jnp.where(match, weights[None, :], jnp.zeros_like(weights)[None, :]), axis=1
    )
    return (chosen.astype(jnp.bfloat16), slot_gate)


def local(grad_out, expert_ids, route_gates, saved_hidden):
    data_count = lax.axis_size("dp")
    expert_count = lax.axis_size("expert")
    chosen, slot_gate = slot_table(expert_ids, route_gates, expert_count)
    width = grad_out.shape[1] * lax.axis_size("tensor")
    block_width = width // data_count
    complete = gathered_copies(grad_out, "tensor", 1)
    parted = complete.reshape(complete.shape[0], data_count, block_width)
    picked = jnp.einsum("st,tdk->dsk", chosen, parted, preferred_element_type=jnp.float32)
    outgoing = (picked * slot_gate[None, :, None]).astype(jnp.bfloat16)
    outgoing = outgoing.reshape(data_count * expert_count, CAP, block_width)
    arrived = lax.all_to_all(outgoing, ("dp", "expert"), split_axis=0, concat_axis=0, tiled=True)
    received = arrived.reshape(-1, block_width)
    hidden = saved_hidden[0]
    summed = lax.dot_general(
        lax.all_gather(hidden, "dp", axis=0, tiled=True),
        received,
        (((0,), (0,)), ((), ())),
        preferred_element_type=jnp.float32,
    )
    return summed.astype(jnp.bfloat16)[None]


def solution(mesh):
    in_specs = (
        P(("dp", "expert"), "tensor"),
        P(("dp", "expert"), None),
        P(("dp", "expert"), None),
        P("expert", "dp", "tensor"),
    )
    out_specs = P("expert", "tensor", "dp")
    return jax.shard_map(local, mesh=mesh, in_specs=in_specs, out_specs=out_specs, check_vma=False)
```

profile of v0, /device:TPU:22, one launch (start us, length us, event | category | flops | bytes accessed | tf_op | source)
XLA Modules:
  0.0 190.3 jit_solution(3089983073668521351)
XLA Ops:
  6.5 1.0 copy.20
  7.6 1.4 broadcast_in_dim.35
  9.0 7.3 %all-to-all-start = ((bf16[16,128,384]{1,2,0:T(8,128)(2,1)}), bf16[16,128,384]{1,2,0:T(8,128)(2,1)S(1)}, u32[]{:S(2)}, u32[]{:S(2)}) async-start(bf16[16,128,384]{1,2,0:T(8,128)(2,1)} %broadcast_in_dim.35), calls=%async_computation | async-start | bytes 3145728 | tf_op jit(solution)/shard_map/all_to_all | solution.py:12
  16.3 0.7 all-gather.3.cloned.1.call-update
  17.0 0.1 copy.15
  17.1 0.1 eq.50
  17.3 0.1 eq.46
  17.4 0.6 reduce-window.6
  18.0 0.2 slice_reduce_fusion
  18.3 0.1 copy.22
  18.4 0.1 broadcast_in_dim.37
  18.5 0.1 fusion.11
  18.6 0.1 reduce_sum.21
  18.8 0.1 copy.18
  18.9 0.1 copy.19
  19.0 0.1 fusion.8
  19.0 0.1 select_reduce_fusion
  19.2 34.6 %all-to-all-done = bf16[16,128,384]{1,2,0:T(8,128)(2,1)S(1)} async-done(((bf16[16,128,384]{1,2,0:T(8,128)(2,1)}), bf16[16,128,384]{1,2,0:T(8,128)(2,1)S(1)}, u32[]{:S(2)}, u32[]{:S(2)}) %all-to-all-start) | async-done | bytes 1572896 | tf_op jit(solution)/shard_map/all_to_all | solution.py:12
  53.7 2.7 %multiply_convert_fusion = bf16[256,8,768]{2,0,1:T(8,128)(2,1)} fusion(f32[256]{0:T(256)S(1)} %select_reduce_fusion, bf16[128,8,768]{0,2,1:T(8,128)(2,1)S(1)} %bitcast.31, pred[256,128]{1,0:T(8,128)(4,1)S(1)} %fusion.8), kind=kOutput, calls=%fused_computation | convolution fusion | flops 405798912 | bytes 4752384 | tf_op jit(solution)/shard_map/st,tdk->dsk/dot_general | solution.py:51
  56.4 23.3 %all-to-all-start.1 = ((bf16[64,32,768]{2,1,0:T(8,128)(2,1)}), bf16[64,32,768]{2,1,0:T(8,128)(2,1)S(1)}, u32[]{:S(2)}, u32[]{:S(2)}) async-start(bf16[64,32,768]{2,1,0:T(8,128)(2,1)} %bitcast.6), calls=%async_computation.1 | async-start | bytes 6291456 | tf_op jit(solution)/shard_map/all_to_all | solution.py:54
  79.7 27.9 %all-gather.3.cloned.1.call-done = bf16[1,2048,1024]{2,1,0:T(8,128)(2,1)} async-done(((bf16[1,256,1024]{2,1,0:T(8,128)(2,1)}), bf16[1,2048,1024]{2,1,0:T(8,128)(2,1)}) %all-gather.3.cloned.1.call-update) | async-done | bytes 4194320 | tf_op jit(solution)/shard_map/all_gather | solution.py:58
  107.7 66.4 %all-to-all-done.1 = bf16[64,32,768]{2,1,0:T(8,128)(2,1)S(1)} async-done(((bf16[64,32,768]{2,1,0:T(8,128)(2,1)}), bf16[64,32,768]{2,1,0:T(8,128)(2,1)S(1)}, u32[]{:S(2)}, u32[]{:S(2)}) %all-to-all-start.1) | async-done | bytes 3145760 | tf_op jit(solution)/shard_map/all_to_all | solution.py:54
  174.1 6.8 %fusion.5 = bf16[1,1024,768]{1,2,0:T(8,128)(2,1)} fusion(bf16[2048,768]{1,0:T(8,128)(2,1)S(1)} %bitcast.32, bf16[1,2048,1024]{2,1,0:T(8,128)(2,1)} %all-gather.3.cloned.1.call-done), kind=kOutput, calls=%fused_computation.4 | convolution fusion | flops 3222011904 | bytes 8912896 | tf_op jit(solution)/shard_map/dot_general | solution.py:57
  180.8 2.6 %copy.23 = bf16[1,1024,768]{2,1,0:T(8,128)(2,1)} copy(bf16[1,1024,768]{1,2,0:T(8,128)(2,1)} %fusion.5) | data formatting | bytes 3145728 | tf_op jit(solution)/shard_map/broadcast_in_dim | solution.py:63
  (11 shorter events, 0.1 us)
Async XLA Ops:
  6.5 10.5 %copy-start = (s32[128,2]{0,1:T(2,128)S(1)}, s32[128,2]{0,1:T(2,128)}, u32[]{:S(2)}) copy-start(s32[128,2]{0,1:T(2,128)} %param.5) | copy-start | bytes 3076
  6.5 11.7 %copy-start.1 = (f32[128,2]{0,1:T(2,128)S(1)}, f32[128,2]{0,1:T(2,128)}, u32[]{:S(2)}) copy-start(f32[128,2]{0,1:T(2,128)} %param.6) | copy-start | bytes 3076
  9.0 44.7 %all-to-all-start = ((bf16[16,128,384]{1,2,0:T(8,128)(2,1)}), bf16[16,128,384]{1,2,0:T(8,128)(2,1)S(1)}, u32[]{:S(2)}, u32[]{:S(2)}) async-start(bf16[16,128,384]{1,2,0:T(8,128)(2,1)} %broadcast_in_dim.35), calls=%async_computation | async-start | bytes 3145728 | tf_op jit(solution)/shard_map/all_to_all | solution.py:12
  16.3 91.4 %all-gather.3.cloned.1.call-start = ((), (), s32[]{:S(2)}) async-start(), calls=%async_computation.2 | async-start | bytes 4718592 | tf_op jit(solution)/shard_map/all_gather | solution.py:58
  56.4 117.7 %all-to-all-start.1 = ((bf16[64,32,768]{2,1,0:T(8,128)(2,1)}), bf16[64,32,768]{2,1,0:T(8,128)(2,1)S(1)}, u32[]{:S(2)}, u32[]{:S(2)}) async-start(bf16[64,32,768]{2,1,0:T(8,128)(2,1)} %bitcast.6), calls=%async_computation.1 | async-start | bytes 6291456 | tf_op jit(solution)/shard_map/all_to_all | solution.py:54
Sparse Core Ops, SparseCore 0:
  19.7 87.8 all-gather.2
where the time goes:
time: 191 us; the launch traced here: 190 us
  waiting for transfers between devices  130 us (68%)
  starting transfers between devices  30.6 us (16%)
  between operations  13.5 us (7%)
  matrix products  9.42 us (5%)
  local copies, waits for them, and re-layouts  6.24 us (3%)
    all_to_all x1, waiting for transfers between devices, local(): lax.all_to_all(outgoing, ('dp', 'expert'), split_axis=0, concat_axis=0, t...  66.4 us
    all_to_all x1, waiting for transfers between devices, from_everyone(): return lax.all_to_all(copies, axis, split_axis=0, concat_axis=0, tiled=True)  34.6 us
    all_gather x1, waiting for transfers between devices, local(): lax.all_gather(hidden, 'dp', axis=0, tiled=True)  27.9 us
    all_to_all x1, starting transfers between devices, local(): lax.all_to_all(outgoing, ('dp', 'expert'), split_axis=0, concat_axis=0, t...  23.3 us
    all_to_all x1, starting transfers between devices, from_everyone(): return lax.all_to_all(copies, axis, split_axis=0, concat_axis=0, tiled=True)  7.25 us
    dot_general x1, matrix products, local(): lax.dot_general(lax.all_gather(hidden, 'dp', axis=0, tiled=True), receive...  6.76 us
  transfers between devices with their start and end apart: 3, of which 3 were waited for; matrix products, arithmetic and copies ran while one was open for 2% of the time, Pallas kernels for 0%

commit v1 on v0

v1 whole, which is shorter than its diff:
```python
import jax
import jax.numpy as jnp
from jax import lax
from jax.experimental import pallas as pl
from jax.experimental.pallas import tpu as pltpu
from jax.sharding import PartitionSpec as P

TOP = 2
CAP = 32
CORES = 2


def slot_table(expert_ids, route_gates, expert_count):
    routes = expert_ids.reshape(-1)
    weights = route_gates.reshape(-1)
    onehot = (routes[:, None] == jnp.arange(expert_count, dtype=jnp.int32)[None, :]).astype(
        jnp.int32
    )
    before = jnp.cumsum(onehot, axis=0) - onehot
    rank = jnp.sum(before * onehot, axis=1)
    target = jnp.where(rank < CAP, routes * CAP + rank, -1)
    match = jnp.arange(expert_count * CAP, dtype=jnp.int32)[:, None] == target[None, :]
    chosen = match.reshape(expert_count * CAP, -1, TOP).any(axis=2)
    slot_gate = jnp.sum(
        jnp.where(match, weights[None, :], jnp.zeros_like(weights)[None, :]), axis=1
    )
    return (chosen.astype(jnp.bfloat16), slot_gate)


def two_way_ring(first, second, axis, up, down, count):
    half = count // 2
    first_up, second_up, first_down, second_down = first, second, first, second
    pairs = []
    for step in range(1, half + 1):
        first_up = lax.ppermute(first_up, axis, up)
        second_down = lax.ppermute(second_down, axis, down)
        if step < half:
            second_up = lax.ppermute(second_up, axis, up)
            first_down = lax.ppermute(first_down, axis, down)
            pairs.append((-step, first_up, second_up))
            pairs.append((step, first_down, second_down))
        else:
            pairs.append((half, first_up, second_down))
    return pairs


def assemble_body(offsets, count, where_ref, own_ref, *rest):
    piece_refs, out_ref = rest[:-1], rest[-1]
    half = own_ref.shape[0] // 2

    def put(j, refs):
        row = pl.multiple_of(j * CAP, CAP)
        for k, ref in enumerate(refs):
            for i in range(ref.shape[0]):
                out_ref[k * half + i, pl.ds(row, CAP), :] = ref[i]

    me = where_ref[0]
    put(me, [own_ref])
    for n, offset in enumerate(offsets):
        put((me + offset) % count, piece_refs[2 * n : 2 * n + 2])


def matmul_body(offsets, count, where_ref, mine_ref, other_ref, hidden_ref, *rest):
    piece_refs, out_ref = rest[:-1], rest[-1]
    width = mine_ref.shape[2]
    me, core = where_ref[0], where_ref[1]
    total = [jnp.zeros((out_ref.shape[0], width), jnp.float32) for _ in range(2)]
    sources = [(0, hidden_ref[...])]
    for n, offset in enumerate(offsets):
        sources.append(
            (offset, jnp.concatenate([r[...] for r in piece_refs[2 * n : 2 * n + 2]], axis=0))
        )
    for offset, hidden in sources:
        i = (me + offset) % count
        for k, ref in enumerate((mine_ref, other_ref)):
            total[k] += lax.dot_general(
                hidden, ref[i], (((0,), (0,)), ((), ())), preferred_element_type=jnp.float32
            )
    for k in range(2):
        column = pl.multiple_of((core if k == 0 else 1 - core) * width, 128)
        out_ref[:, pl.ds(column, width)] = total[k].astype(out_ref.dtype)


def whole(array):
    return pl.BlockSpec(array.shape, lambda *_: (0,) * array.ndim)


def local(grad_out, expert_ids, route_gates, saved_hidden):
    data_count = lax.axis_size("dp")
    expert_count = lax.axis_size("expert")
    tensor_count = lax.axis_size("tensor")
    chips = tensor_count // CORES
    hidden = saved_hidden[0]
    rows, units = hidden.shape
    y_up = [(k, (k + 1) % data_count) for k in range(data_count)]
    y_down = [(k, (k - 1) % data_count) for k in range(data_count)]
    x_up = [(k, (k + CORES) % tensor_count) for k in range(tensor_count)]
    x_down = [(k, (k - CORES) % tensor_count) for k in range(tensor_count)]
    swap = [(k, k ^ 1) for k in range(tensor_count)]
    same_core = [[c + CORES * k for k in range(chips)] for c in range(CORES)]

    hidden_pairs = two_way_ring(
        hidden[: rows // 2], hidden[rows // 2 :], "dp", y_up, y_down, data_count
    )

    chosen, slot_gate = slot_table(expert_ids, route_gates, expert_count)
    picked = jnp.dot(chosen, grad_out, preferred_element_type=jnp.float32)
    slots = (picked * slot_gate[:, None]).astype(jnp.bfloat16)
    slots = slots.reshape(expert_count, CAP, grad_out.shape[1])
    slots = lax.all_to_all(slots, "expert", 0, 0, tiled=True)
    slots = lax.all_to_all(slots, "tensor", 0, 0, tiled=True, axis_index_groups=same_core)
    slots = lax.all_to_all(slots, "dp", 0, 0, tiled=True)
    width = slots.shape[2]
    slot_pairs = two_way_ring(
        slots[: data_count // 2], slots[data_count // 2 :], "tensor", x_up, x_down, chips
    )
    y = lax.axis_index("dp")
    t = lax.axis_index("tensor")
    x, core = t // CORES, t % CORES
    place = jnp.stack([x, core]).astype(jnp.int32)
    pieces = [p for pair in slot_pairs for p in pair[1:]]
    shape = jax.ShapeDtypeStruct((data_count, chips * CAP, width), jnp.bfloat16)
    smem = pl.BlockSpec(memory_space=pltpu.SMEM)
    mine = pl.pallas_call(
        lambda *refs: assemble_body([p[0] for p in slot_pairs], chips, *refs),
        out_shape=shape,
        in_specs=[smem] + [whole(a) for a in [slots, *pieces]],
        out_specs=whole(shape),
        name="assemble",
    )(place, slots, *pieces)
    other = lax.ppermute(mine, "tensor", swap)

    place = jnp.stack([y, core]).astype(jnp.int32)
    pieces = [p for pair in hidden_pairs for p in pair[1:]]
    block = 256
    out = pl.pallas_call(
        lambda *refs: matmul_body([p[0] for p in hidden_pairs], data_count, *refs),
        out_shape=jax.ShapeDtypeStruct((units, CORES * width), jnp.bfloat16),
        grid=(units // block,),
        in_specs=[smem, whole(mine), whole(other)]
        + [pl.BlockSpec((a.shape[0], block), lambda g: (0, g)) for a in [hidden, *pieces]],
        out_specs=pl.BlockSpec((block, CORES * width), lambda g: (g, 0)),
        name="matmul",
    )(place, mine, other, hidden, *pieces)
    return out[None]


def solution(mesh):
    in_specs = (
        P(("dp", "expert"), "tensor"),
        P(("dp", "expert"), None),
        P(("dp", "expert"), None),
        P("expert", "dp", "tensor"),
    )
    out_specs = P("expert", "tensor", "dp")
    return jax.shard_map(local, mesh=mesh, in_specs=in_specs, out_specs=out_specs, check_vma=False)
```

time: 191 us -> 182 us (0.953)
  the two profiles are of different devices: /device:TPU:22 before, /device:TPU:1 now
where the time goes in v1:
time: 182 us; the launch traced here: 180 us
  starting transfers between devices  91.9 us (50%)
  blocking collectives  56.8 us (31%)
  waiting for transfers between devices  11.5 us (6%)
  Pallas kernels  11.3 us (6%)
  local copies, waits for them, and re-layouts  4.38 us (2%)
  other arithmetic  2.86 us (2%)
    ppermute x6, starting transfers between devices, two_way_ring(): first_down = lax.ppermute(first_down, axis, down)  27.1 us
    all_to_all x1, blocking collectives, local(): slots = lax.all_to_all(slots, 'expert', 0, 0, tiled=True)  26 us
    ppermute x8, starting transfers between devices, two_way_ring(): first_up = lax.ppermute(first_up, axis, up)  24.9 us
    ppermute x8, starting transfers between devices, two_way_ring(): second_down = lax.ppermute(second_down, axis, down)  17.6 us
    all_to_all x1, blocking collectives, local(): slots = lax.all_to_all(slots, 'dp', 0, 0, tiled=True)  15.8 us
    all_to_all x1, blocking collectives, local(): lax.all_to_all(slots, 'tensor', 0, 0, tiled=True, axis_index_groups=same_...  15 us
    ppermute x6, starting transfers between devices, two_way_ring(): second_up = lax.ppermute(second_up, axis, up)  11.8 us
    ppermute x1, starting transfers between devices, local(): other = lax.ppermute(mine, 'tensor', swap)  10.5 us
  transfers between devices with their start and end apart: 29, of which 4 were waited for; matrix products, arithmetic and copies ran while one was open for 1% of the time, Pallas kernels for 0%

profile of v1, /device:TPU:1, one launch (start us, length us, event | category | flops | bytes accessed | tf_op | source)
XLA Modules:
  0.0 179.8 jit_solution(11574538577970493759)
XLA Ops:
  4.4 26.0 %all_to_all.15 = bf16[8,32,384]{2,1,0:T(8,128)(2,1)S(1)} all-to-all(bf16[8,32,384]{2,1,0:T(8,128)(2,1)S(1)} %bitcast.21), channel_id=1, replica_groups=mesh['dp'=8,'expert'=8,'tensor'=16] {'expert'}, dimensions={0} | all-to-all | bytes 393216 | tf_op jit(solution)/shard_map/all_to_all | solution.py:110
  30.4 15.0 %all_to_all.16 = bf16[8,32,384]{2,1,0:T(8,128)(2,1)S(1)} all-to-all(bf16[8,32,384]{2,1,0:T(8,128)(2,1)S(1)} %all_to_all.15), channel_id=1, replica_groups={{0,2,4,6,8,10,12,14},{1,3,5,7,9,11,13,15},{16,18,20,22,24,26,28,30},{17..., dimensions={0} | all-to-all | bytes 393216 | tf_op jit(solution)/shard_map/all_to_all | solution.py:111
  45.4 15.8 %all_to_all.17.refs_1_ = bf16[8,32,384]{2,1,0:T(8,128)(2,1)S(1)} all-to-all(bf16[8,32,384]{2,1,0:T(8,128)(2,1)S(1)} %all_to_all.16), channel_id=1, replica_groups=mesh['dp'=8,'expert'=8,'tensor'=16] {'dp'}, dimensions={0} | all-to-all | bytes 393216 | tf_op jit(solution)/shard_map/all_to_all | solution.py:112
  63.2 3.4 %collective-permute-start = (bf16[4,32,384]{2,1,0:T(8,128)(2,1)S(1)}, bf16[4,32,384]{2,1,0:T(8,128)(2,1)S(1)}, u32[]{:S(2)}, u32[]{:S(2)}) collective-permute-start(bf16[4,32,384]{2,1,0:T(8,128)(2,1)S(1)} %get-tuple-element.8), channel_id=1, source_target_pairs={{0,2},{1,3},{2,4},{3,5},{4,6},{5,7},{6,8},{7,9},{8,10},{9,11},{10,... | collective-permute-start | bytes 294920 | tf_op jit(solution)/shard_map/ppermute | solution.py:35
  68.5 4.5 %collective-permute-start.2 = (bf16[4,32,384]{2,1,0:T(8,128)(2,1)S(1)}, bf16[4,32,384]{2,1,0:T(8,128)(2,1)S(1)}, u32[]{:S(2)}, u32[]{:S(2)}) collective-permute-start(bf16[4,32,384]{2,1,0:T(8,128)(2,1)S(1)} %get-tuple-element.8), channel_id=1, source_target_pairs={{0,14},{1,15},{2,0},{3,1},{4,2},{5,3},{6,4},{7,5},{8,6},{9,7},{10,... | collective-permute-start | bytes 294920 | tf_op jit(solution)/shard_map/ppermute | solution.py:39
  75.0 3.4 %collective-permute-start.4 = (bf16[4,32,384]{2,1,0:T(8,128)(2,1)S(1)}, bf16[4,32,384]{2,1,0:T(8,128)(2,1)S(1)}, u32[]{:S(2)}, u32[]{:S(2)}) collective-permute-start(bf16[4,32,384]{2,1,0:T(8,128)(2,1)S(1)} %collective-permute-done.refs_2_), channel_id=1, source_target_pairs={{0,2},{1,3},{2,4},{3,5},{4,6},{5,7},{6,8},{7,9},{8,10},{9,11},{10,... | collective-permute-start | bytes 294920 | tf_op jit(solution)/shard_map/ppermute | solution.py:35
  80.3 4.6 %collective-permute-start.6 = (bf16[4,32,384]{2,1,0:T(8,128)(2,1)S(1)}, bf16[4,32,384]{2,1,0:T(8,128)(2,1)S(1)}, u32[]{:S(2)}, u32[]{:S(2)}) collective-permute-start(bf16[4,32,384]{2,1,0:T(8,128)(2,1)S(1)} %collective-permute-done.2.refs_4_), channel_id=1, source_target_pairs={{0,14},{1,15},{2,0},{3,1},{4,2},{5,3},{6,4},{7,5},{8,6},{9,7},{10,... | collective-permute-start | bytes 294920 | tf_op jit(solution)/shard_map/ppermute | solution.py:39
  86.9 3.4 %collective-permute-start.8 = (bf16[4,32,384]{2,1,0:T(8,128)(2,1)S(1)}, bf16[4,32,384]{2,1,0:T(8,128)(2,1)S(1)}, u32[]{:S(2)}, u32[]{:S(2)}) collective-permute-start(bf16[4,32,384]{2,1,0:T(8,128)(2,1)S(1)} %collective-permute-done.4.refs_6_), channel_id=1, source_target_pairs={{0,2},{1,3},{2,4},{3,5},{4,6},{5,7},{6,8},{7,9},{8,10},{9,11},{10,... | collective-permute-start | bytes 294920 | tf_op jit(solution)/shard_map/ppermute | solution.py:35
  92.3 4.6 %collective-permute-start.10 = (bf16[4,32,384]{2,1,0:T(8,128)(2,1)S(1)}, bf16[4,32,384]{2,1,0:T(8,128)(2,1)S(1)}, u32[]{:S(2)}, u32[]{:S(2)}) collective-permute-start(bf16[4,32,384]{2,1,0:T(8,128)(2,1)S(1)} %collective-permute-done.6.refs_8_), channel_id=1, source_target_pairs={{0,14},{1,15},{2,0},{3,1},{4,2},{5,3},{6,4},{7,5},{8,6},{9,7},{10,... | collective-permute-start | bytes 294920 | tf_op jit(solution)/shard_map/ppermute | solution.py:39
  98.8 3.4 %collective-permute-start.12 = (bf16[4,32,384]{2,1,0:T(8,128)(2,1)S(1)}, bf16[4,32,384]{2,1,0:T(8,128)(2,1)S(1)}, u32[]{:S(2)}, u32[]{:S(2)}) collective-permute-start(bf16[4,32,384]{2,1,0:T(8,128)(2,1)S(1)} %collective-permute-done.8.refs_10_), channel_id=1, source_target_pairs={{0,2},{1,3},{2,4},{3,5},{4,6},{5,7},{6,8},{7,9},{8,10},{9,11},{10,... | collective-permute-start | bytes 294920 | tf_op jit(solution)/shard_map/ppermute | solution.py:35
  102.8 3.6 %collective-permute-done.12.refs_14_ = bf16[4,32,384]{2,1,0:T(8,128)(2,1)S(1)} collective-permute-done((bf16[4,32,384]{2,1,0:T(8,128)(2,1)S(1)}, bf16[4,32,384]{2,1,0:T(8,128)(2,1)S(1)}, u32[]{:S(2)}, u32[]{:S(2)}) %collective-permute-start.12) | collective-permute-done | bytes 98336 | tf_op jit(solution)/shard_map/ppermute | solution.py:35
  107.2 2.8 %assemble.1.refs_1_ = bf16[8,256,384]{2,1,0:T(8,128)(2,1)} custom-call(s32[2]{0:T(128)} %pad_add_fusion.1.refs_0_, bf16[8,32,384]{2,1,0:T(8,128)(2,1)} %copy-done.2, bf16[4,32,384]{2,1,0:T(8,128)(2,1)} %copy-done.12, bf16[4,32,384]{2,1,0:T(8,128)(2,1)} %copy-done.13, bf16[4,32,384]{2,1,0:T(8,128)(2,1)} %copy-done.14, bf16[4,32,384]{2,1,0:T(8,128)(2,1)} %copy-done.11, ...), custom_call_target="tpu_custom_call" | custom-call | tf_op jit(solution)/shard_map/assemble/pallas_call | solution.py:124
  110.0 10.5 %collective-permute-start.14 = (bf16[8,256,384]{2,1,0:T(8,128)(2,1)}, bf16[8,256,384]{2,1,0:T(8,128)(2,1)S(1)}, u32[]{:S(2)}, u32[]{:S(2)}) collective-permute-start(bf16[8,256,384]{2,1,0:T(8,128)(2,1)} %assemble.1.refs_1_), channel_id=1, source_target_pairs={{0,1},{1,0},{2,3},{3,2},{4,5},{5,4},{6,7},{7,6},{8,9},{9,8},{10,11... | collective-permute-start | bytes 4718600 | tf_op jit(solution)/shard_map/ppermute | solution.py:131
  122.5 3.4 %collective-permute-start.15 = (bf16[128,1024]{1,0:T(8,128)(2,1)S(1)}, bf16[128,1024]{1,0:T(8,128)(2,1)S(1)}, u32[]{:S(2)}, u32[]{:S(2)}) collective-permute-start(bf16[128,1024]{1,0:T(8,128)(2,1)S(1)} %get-tuple-element.6), channel_id=1, source_target_pairs={{0,128},{128,256},{256,384},{384,512},{512,640},{640,768},{768,896... | collective-permute-start | bytes 786440 | tf_op jit(solution)/shard_map/ppermute | solution.py:35
  128.0 4.3 %collective-permute-start.17 = (bf16[128,1024]{1,0:T(8,128)(2,1)S(1)}, bf16[128,1024]{1,0:T(8,128)(2,1)S(1)}, u32[]{:S(2)}, u32[]{:S(2)}) collective-permute-start(bf16[128,1024]{1,0:T(8,128)(2,1)S(1)} %get-tuple-element.6), channel_id=1, source_target_pairs={{0,896},{128,0},{256,128},{384,256},{512,384},{640,512},{768,640},... | collective-permute-start | bytes 786440 | tf_op jit(solution)/shard_map/ppermute | solution.py:39
  134.3 3.4 %collective-permute-start.19 = (bf16[128,1024]{1,0:T(8,128)(2,1)S(1)}, bf16[128,1024]{1,0:T(8,128)(2,1)S(1)}, u32[]{:S(2)}, u32[]{:S(2)}) collective-permute-start(bf16[128,1024]{1,0:T(8,128)(2,1)S(1)} %collective-permute-done.15.refs_4_), channel_id=1, source_target_pairs={{0,128},{128,256},{256,384},{384,512},{512,640},{640,768},{768,896... | collective-permute-start | bytes 786440 | tf_op jit(solution)/shard_map/ppermute | solution.py:35
  141.0 4.6 %collective-permute-start.21 = (bf16[128,1024]{1,0:T(8,128)(2,1)S(1)}, bf16[128,1024]{1,0:T(8,128)(2,1)}, u32[]{:S(2)}, u32[]{:S(2)}) collective-permute-start(bf16[128,1024]{1,0:T(8,128)(2,1)S(1)} %collective-permute-done.17.refs_6_), channel_id=1, source_target_pairs={{0,896},{128,0},{256,128},{384,256},{512,384},{640,512},{768,640},... | collective-permute-start | bytes 786440 | tf_op jit(solution)/shard_map/ppermute | solution.py:39
  145.6 2.5 %collective-permute-start.26 = (bf16[128,1024]{1,0:T(8,128)(2,1)S(1)}, bf16[128,1024]{1,0:T(8,128)(2,1)}, u32[]{:S(2)}, u32[]{:S(2)}) collective-permute-start(bf16[128,1024]{1,0:T(8,128)(2,1)S(1)} %collective-permute-done.22.refs_11_), channel_id=1, source_target_pairs={{0,896},{128,0},{256,128},{384,256},{512,384},{640,512},{768,640},... | collective-permute-start | bytes 786440 | tf_op jit(solution)/shard_map/ppermute | solution.py:36
  148.1 2.8 %collective-permute-start.23 = (bf16[128,1024]{1,0:T(8,128)(2,1)S(1)}, bf16[128,1024]{1,0:T(8,128)(2,1)}, u32[]{:S(2)}, u32[]{:S(2)}) collective-permute-start(bf16[128,1024]{1,0:T(8,128)(2,1)S(1)} %collective-permute-done.19.refs_8_), channel_id=1, source_target_pairs={{0,128},{128,256},{256,384},{384,512},{512,640},{640,768},{768,896... | collective-permute-start | bytes 786440 | tf_op jit(solution)/shard_map/ppermute | solution.py:35
  152.9 4.6 %collective-permute-start.25 = (bf16[128,1024]{1,0:T(8,128)(2,1)}, bf16[128,1024]{1,0:T(8,128)(2,1)}, u32[]{:S(2)}, u32[]{:S(2)}) collective-permute-start(bf16[128,1024]{1,0:T(8,128)(2,1)} %collective-permute-done.21.refs_10_), channel_id=1, source_target_pairs={{0,896},{128,0},{256,128},{384,256},{512,384},{640,512},{768,640},... | collective-permute-start | bytes 786440 | tf_op jit(solution)/shard_map/ppermute | solution.py:39
  157.4 3.6 %collective-permute-start.28 = (bf16[128,1024]{1,0:T(8,128)(2,1)}, bf16[128,1024]{1,0:T(8,128)(2,1)}, u32[]{:S(2)}, u32[]{:S(2)}) collective-permute-start(bf16[128,1024]{1,0:T(8,128)(2,1)} %collective-permute-done.26.refs_15_), channel_id=1, source_target_pairs={{0,896},{128,0},{256,128},{384,256},{512,384},{640,512},{768,640},... | collective-permute-start | bytes 786440 | tf_op jit(solution)/shard_map/ppermute | solution.py:36
  163.7 3.8 %collective-permute-done.28.refs_17_ = bf16[128,1024]{1,0:T(8,128)(2,1)} collective-permute-done((bf16[128,1024]{1,0:T(8,128)(2,1)}, bf16[128,1024]{1,0:T(8,128)(2,1)}, u32[]{:S(2)}, u32[]{:S(2)}) %collective-permute-start.28) | collective-permute-done | bytes 262176 | tf_op jit(solution)/shard_map/ppermute | solution.py:36
  167.5 2.6 %collective-permute-done.27.refs_16_ = bf16[128,1024]{1,0:T(8,128)(2,1)} collective-permute-done((bf16[128,1024]{1,0:T(8,128)(2,1)}, bf16[128,1024]{1,0:T(8,128)(2,1)}, u32[]{:S(2)}, u32[]{:S(2)}) %collective-permute-start.27) | collective-permute-done | bytes 262176 | tf_op jit(solution)/shard_map/ppermute | solution.py:35
  171.3 8.5 %matmul.1 = bf16[1024,768]{1,0:T(8,128)(2,1)} custom-call(s32[2]{0:T(128)} %pad_add_fusion.refs_0_, bf16[8,256,384]{2,1,0:T(8,128)(2,1)} %assemble.1.refs_1_, bf16[8,256,384]{2,1,0:T(8,128)(2,1)} %copy-done.3, bf16[256,1024]{1,0:T(8,128)(2,1)} %bitcast.20, bf16[128,1024]{1,0:T(8,128)(2,1)} %copy-done.5, bf16[128,1024]{1,0:T(8,128)(2,1)} %copy-done.6, ...), custom_call_target="tpu_custom_call" | custom-call | tf_op jit(solution)/shard_map/matmul/pallas_call | solution.py:136
  (113 shorter events, 34.1 us)
Async XLA Ops:
  61.2 11.8 %collective-permute-start.3 = (bf16[4,32,384]{2,1,0:T(8,128)(2,1)S(1)}, bf16[4,32,384]{2,1,0:T(8,128)(2,1)S(1)}, u32[]{:S(2)}, u32[]{:S(2)}) collective-permute-start(bf16[4,32,384]{2,1,0:T(8,128)(2,1)S(1)} %get-tuple-element.7), channel_id=1, source_target_pairs={{0,14},{1,15},{2,0},{3,1},{4,2},{5,3},{6,4},{7,5},{8,6},{9,7},{10,... | collective-permute-start | bytes 294920 | tf_op jit(solution)/shard_map/ppermute | solution.py:36
  63.2 11.8 %collective-permute-start = (bf16[4,32,384]{2,1,0:T(8,128)(2,1)S(1)}, bf16[4,32,384]{2,1,0:T(8,128)(2,1)S(1)}, u32[]{:S(2)}, u32[]{:S(2)}) collective-permute-start(bf16[4,32,384]{2,1,0:T(8,128)(2,1)S(1)} %get-tuple-element.8), channel_id=1, source_target_pairs={{0,2},{1,3},{2,4},{3,5},{4,6},{5,7},{6,8},{7,9},{8,10},{9,11},{10,... | collective-permute-start | bytes 294920 | tf_op jit(solution)/shard_map/ppermute | solution.py:35
  66.5 11.9 %collective-permute-start.1 = (bf16[4,32,384]{2,1,0:T(8,128)(2,1)S(1)}, bf16[4,32,384]{2,1,0:T(8,128)(2,1)S(1)}, u32[]{:S(2)}, u32[]{:S(2)}) collective-permute-start(bf16[4,32,384]{2,1,0:T(8,128)(2,1)S(1)} %get-tuple-element.7), channel_id=1, source_target_pairs={{0,2},{1,3},{2,4},{3,5},{4,6},{5,7},{6,8},{7,9},{8,10},{9,11},{10,... | collective-permute-start | bytes 294920 | tf_op jit(solution)/shard_map/ppermute | solution.py:38
  68.5 11.8 %collective-permute-start.2 = (bf16[4,32,384]{2,1,0:T(8,128)(2,1)S(1)}, bf16[4,32,384]{2,1,0:T(8,128)(2,1)S(1)}, u32[]{:S(2)}, u32[]{:S(2)}) collective-permute-start(bf16[4,32,384]{2,1,0:T(8,128)(2,1)S(1)} %get-tuple-element.8), channel_id=1, source_target_pairs={{0,14},{1,15},{2,0},{3,1},{4,2},{5,3},{6,4},{7,5},{8,6},{9,7},{10,... | collective-permute-start | bytes 294920 | tf_op jit(solution)/shard_map/ppermute | solution.py:39
  73.1 11.9 %collective-permute-start.7 = (bf16[4,32,384]{2,1,0:T(8,128)(2,1)S(1)}, bf16[4,32,384]{2,1,0:T(8,128)(2,1)S(1)}, u32[]{:S(2)}, u32[]{:S(2)}) collective-permute-start(bf16[4,32,384]{2,1,0:T(8,128)(2,1)S(1)} %collective-permute-done.3.refs_5_), channel_id=1, source_target_pairs={{0,14},{1,15},{2,0},{3,1},{4,2},{5,3},{6,4},{7,5},{8,6},{9,7},{10,... | collective-permute-start | bytes 294920 | tf_op jit(solution)/shard_map/ppermute | solution.py:36
  75.0 11.9 %collective-permute-start.4 = (bf16[4,32,384]{2,1,0:T(8,128)(2,1)S(1)}, bf16[4,32,384]{2,1,0:T(8,128)(2,1)S(1)}, u32[]{:S(2)}, u32[]{:S(2)}) collective-permute-start(bf16[4,32,384]{2,1,0:T(8,128)(2,1)S(1)} %collective-permute-done.refs_2_), channel_id=1, source_target_pairs={{0,2},{1,3},{2,4},{3,5},{4,6},{5,7},{6,8},{7,9},{8,10},{9,11},{10,... | collective-permute-start | bytes 294920 | tf_op jit(solution)/shard_map/ppermute | solution.py:35
  78.4 11.9 %collective-permute-start.5 = (bf16[4,32,384]{2,1,0:T(8,128)(2,1)S(1)}, bf16[4,32,384]{2,1,0:T(8,128)(2,1)S(1)}, u32[]{:S(2)}, u32[]{:S(2)}) collective-permute-start(bf16[4,32,384]{2,1,0:T(8,128)(2,1)S(1)} %collective-permute-done.1.refs_3_), channel_id=1, source_target_pairs={{0,2},{1,3},{2,4},{3,5},{4,6},{5,7},{6,8},{7,9},{8,10},{9,11},{10,... | collective-permute-start | bytes 294920 | tf_op jit(solution)/shard_map/ppermute | solution.py:38
  80.3 11.9 %collective-permute-start.6 = (bf16[4,32,384]{2,1,0:T(8,128)(2,1)S(1)}, bf16[4,32,384]{2,1,0:T(8,128)(2,1)S(1)}, u32[]{:S(2)}, u32[]{:S(2)}) collective-permute-start(bf16[4,32,384]{2,1,0:T(8,128)(2,1)S(1)} %collective-permute-done.2.refs_4_), channel_id=1, source_target_pairs={{0,14},{1,15},{2,0},{3,1},{4,2},{5,3},{6,4},{7,5},{8,6},{9,7},{10,... | collective-permute-start | bytes 294920 | tf_op jit(solution)/shard_map/ppermute | solution.py:39
  84.9 11.9 %collective-permute-start.11 = (bf16[4,32,384]{2,1,0:T(8,128)(2,1)S(1)}, bf16[4,32,384]{2,1,0:T(8,128)(2,1)S(1)}, u32[]{:S(2)}, u32[]{:S(2)}) collective-permute-start(bf16[4,32,384]{2,1,0:T(8,128)(2,1)S(1)} %collective-permute-done.7.refs_9_), channel_id=1, source_target_pairs={{0,14},{1,15},{2,0},{3,1},{4,2},{5,3},{6,4},{7,5},{8,6},{9,7},{10,... | collective-permute-start | bytes 294920 | tf_op jit(solution)/shard_map/ppermute | solution.py:36
  86.9 11.9 %collective-permute-start.8 = (bf16[4,32,384]{2,1,0:T(8,128)(2,1)S(1)}, bf16[4,32,384]{2,1,0:T(8,128)(2,1)S(1)}, u32[]{:S(2)}, u32[]{:S(2)}) collective-permute-start(bf16[4,32,384]{2,1,0:T(8,128)(2,1)S(1)} %collective-permute-done.4.refs_6_), channel_id=1, source_target_pairs={{0,2},{1,3},{2,4},{3,5},{4,6},{5,7},{6,8},{7,9},{8,10},{9,11},{10,... | collective-permute-start | bytes 294920 | tf_op jit(solution)/shard_map/ppermute | solution.py:35
  90.3 12.5 %collective-permute-start.9 = (bf16[4,32,384]{2,1,0:T(8,128)(2,1)S(1)}, bf16[4,32,384]{2,1,0:T(8,128)(2,1)S(1)}, u32[]{:S(2)}, u32[]{:S(2)}) collective-permute-start(bf16[4,32,384]{2,1,0:T(8,128)(2,1)S(1)} %collective-permute-done.5.refs_7_), channel_id=1, source_target_pairs={{0,2},{1,3},{2,4},{3,5},{4,6},{5,7},{6,8},{7,9},{8,10},{9,11},{10,... | collective-permute-start | bytes 294920 | tf_op jit(solution)/shard_map/ppermute | solution.py:38
  110.0 60.1 %collective-permute-start.14 = (bf16[8,256,384]{2,1,0:T(8,128)(2,1)}, bf16[8,256,384]{2,1,0:T(8,128)(2,1)S(1)}, u32[]{:S(2)}, u32[]{:S(2)}) collective-permute-start(bf16[8,256,384]{2,1,0:T(8,128)(2,1)} %assemble.1.refs_1_), channel_id=1, source_target_pairs={{0,1},{1,0},{2,3},{3,2},{4,5},{5,4},{6,7},{7,6},{8,9},{9,8},{10,11... | collective-permute-start | bytes 4718600 | tf_op jit(solution)/shard_map/ppermute | solution.py:131
  120.5 11.8 %collective-permute-start.18 = (bf16[128,1024]{1,0:T(8,128)(2,1)S(1)}, bf16[128,1024]{1,0:T(8,128)(2,1)S(1)}, u32[]{:S(2)}, u32[]{:S(2)}) collective-permute-start(bf16[128,1024]{1,0:T(8,128)(2,1)S(1)} %get-tuple-element.5), channel_id=1, source_target_pairs={{0,896},{128,0},{256,128},{384,256},{512,384},{640,512},{768,640},... | collective-permute-start | bytes 786440 | tf_op jit(solution)/shard_map/ppermute | solution.py:36
  122.5 11.8 %collective-permute-start.15 = (bf16[128,1024]{1,0:T(8,128)(2,1)S(1)}, bf16[128,1024]{1,0:T(8,128)(2,1)S(1)}, u32[]{:S(2)}, u32[]{:S(2)}) collective-permute-start(bf16[128,1024]{1,0:T(8,128)(2,1)S(1)} %get-tuple-element.6), channel_id=1, source_target_pairs={{0,128},{128,256},{256,384},{384,512},{512,640},{640,768},{768,896... | collective-permute-start | bytes 786440 | tf_op jit(solution)/shard_map/ppermute | solution.py:35
  125.8 13.2 %collective-permute-start.16 = (bf16[128,1024]{1,0:T(8,128)(2,1)S(1)}, bf16[128,1024]{1,0:T(8,128)(2,1)S(1)}, u32[]{:S(2)}, u32[]{:S(2)}) collective-permute-start(bf16[128,1024]{1,0:T(8,128)(2,1)S(1)} %get-tuple-element.5), channel_id=1, source_target_pairs={{0,128},{128,256},{256,384},{384,512},{512,640},{640,768},{768,896... | collective-permute-start | bytes 786440 | tf_op jit(solution)/shard_map/ppermute | solution.py:38
  128.0 12.9 %collective-permute-start.17 = (bf16[128,1024]{1,0:T(8,128)(2,1)S(1)}, bf16[128,1024]{1,0:T(8,128)(2,1)S(1)}, u32[]{:S(2)}, u32[]{:S(2)}) collective-permute-start(bf16[128,1024]{1,0:T(8,128)(2,1)S(1)} %get-tuple-element.6), channel_id=1, source_target_pairs={{0,896},{128,0},{256,128},{384,256},{512,384},{640,512},{768,640},... | collective-permute-start | bytes 786440 | tf_op jit(solution)/shard_map/ppermute | solution.py:39
  132.4 13.2 %collective-permute-start.22 = (bf16[128,1024]{1,0:T(8,128)(2,1)S(1)}, bf16[128,1024]{1,0:T(8,128)(2,1)S(1)}, u32[]{:S(2)}, u32[]{:S(2)}) collective-permute-start(bf16[128,1024]{1,0:T(8,128)(2,1)S(1)} %collective-permute-done.18.refs_7_), channel_id=1, source_target_pairs={{0,896},{128,0},{256,128},{384,256},{512,384},{640,512},{768,640},... | collective-permute-start | bytes 786440 | tf_op jit(solution)/shard_map/ppermute | solution.py:36
  134.3 13.8 %collective-permute-start.19 = (bf16[128,1024]{1,0:T(8,128)(2,1)S(1)}, bf16[128,1024]{1,0:T(8,128)(2,1)S(1)}, u32[]{:S(2)}, u32[]{:S(2)}) collective-permute-start(bf16[128,1024]{1,0:T(8,128)(2,1)S(1)} %collective-permute-done.15.refs_4_), channel_id=1, source_target_pairs={{0,128},{128,256},{256,384},{384,512},{512,640},{640,768},{768,896... | collective-permute-start | bytes 786440 | tf_op jit(solution)/shard_map/ppermute | solution.py:35
  139.0 11.9 %collective-permute-start.20 = (bf16[128,1024]{1,0:T(8,128)(2,1)S(1)}, bf16[128,1024]{1,0:T(8,128)(2,1)S(1)}, u32[]{:S(2)}, u32[]{:S(2)}) collective-permute-start(bf16[128,1024]{1,0:T(8,128)(2,1)S(1)} %collective-permute-done.16.refs_5_), channel_id=1, source_target_pairs={{0,128},{128,256},{256,384},{384,512},{512,640},{640,768},{768,896... | collective-permute-start | bytes 786440 | tf_op jit(solution)/shard_map/ppermute | solution.py:38
  141.0 11.9 %collective-permute-start.21 = (bf16[128,1024]{1,0:T(8,128)(2,1)S(1)}, bf16[128,1024]{1,0:T(8,128)(2,1)}, u32[]{:S(2)}, u32[]{:S(2)}) collective-permute-start(bf16[128,1024]{1,0:T(8,128)(2,1)S(1)} %collective-permute-done.17.refs_6_), channel_id=1, source_target_pairs={{0,896},{128,0},{256,128},{384,256},{512,384},{640,512},{768,640},... | collective-permute-start | bytes 786440 | tf_op jit(solution)/shard_map/ppermute | solution.py:39
  145.6 11.9 %collective-permute-start.26 = (bf16[128,1024]{1,0:T(8,128)(2,1)S(1)}, bf16[128,1024]{1,0:T(8,128)(2,1)}, u32[]{:S(2)}, u32[]{:S(2)}) collective-permute-start(bf16[128,1024]{1,0:T(8,128)(2,1)S(1)} %collective-permute-done.22.refs_11_), channel_id=1, source_target_pairs={{0,896},{128,0},{256,128},{384,256},{512,384},{640,512},{768,640},... | collective-permute-start | bytes 786440 | tf_op jit(solution)/shard_map/ppermute | solution.py:36
  148.1 13.0 %collective-permute-start.23 = (bf16[128,1024]{1,0:T(8,128)(2,1)S(1)}, bf16[128,1024]{1,0:T(8,128)(2,1)}, u32[]{:S(2)}, u32[]{:S(2)}) collective-permute-start(bf16[128,1024]{1,0:T(8,128)(2,1)S(1)} %collective-permute-done.19.refs_8_), channel_id=1, source_target_pairs={{0,128},{128,256},{256,384},{384,512},{512,640},{640,768},{768,896... | collective-permute-start | bytes 786440 | tf_op jit(solution)/shard_map/ppermute | solution.py:35
  150.9 12.8 %collective-permute-start.24 = (bf16[128,1024]{1,0:T(8,128)(2,1)S(1)}, bf16[128,1024]{1,0:T(8,128)(2,1)}, u32[]{:S(2)}, u32[]{:S(2)}) collective-permute-start(bf16[128,1024]{1,0:T(8,128)(2,1)S(1)} %collective-permute-done.20.refs_9_), channel_id=1, source_target_pairs={{0,128},{128,256},{256,384},{384,512},{512,640},{640,768},{768,896... | collective-permute-start | bytes 786440 | tf_op jit(solution)/shard_map/ppermute | solution.py:38
  152.9 10.8 %collective-permute-start.25 = (bf16[128,1024]{1,0:T(8,128)(2,1)}, bf16[128,1024]{1,0:T(8,128)(2,1)}, u32[]{:S(2)}, u32[]{:S(2)}) collective-permute-start(bf16[128,1024]{1,0:T(8,128)(2,1)} %collective-permute-done.21.refs_10_), channel_id=1, source_target_pairs={{0,896},{128,0},{256,128},{384,256},{512,384},{640,512},{768,640},... | collective-permute-start | bytes 786440 | tf_op jit(solution)/shard_map/ppermute | solution.py:39
  (30 other events, 531.0 us)

commit v2 on v0

v2 whole, which is shorter than its diff:
```python
import jax
import jax.numpy as jnp
from jax import lax
from jax.experimental import pallas as pl
from jax.experimental.pallas import tpu as pltpu
from jax.sharding import PartitionSpec as P

CAP = 32
CORES = 2


def select_body(experts, ids_ref, gates_ref, grads_ref, out_ref):
    tokens = ids_ref.shape[1]
    ids, gates = ids_ref[...], gates_ref[...]
    expert = lax.broadcasted_iota(jnp.int32, (experts, tokens), 0)
    named = jnp.zeros((experts, tokens), jnp.float32)
    gate = jnp.zeros((experts, tokens), jnp.float32)
    for k in range(ids_ref.shape[0]):
        hit = ids[k : k + 1, :] == expert
        named = jnp.where(hit, 1.0, named)
        gate = jnp.where(hit, gates[k : k + 1, :], gate)
    earlier = lax.broadcasted_iota(jnp.int32, (tokens, tokens), 0) < lax.broadcasted_iota(
        jnp.int32, (tokens, tokens), 1
    )
    rank = lax.dot_general(
        named.astype(jnp.bfloat16),
        earlier.astype(jnp.bfloat16),
        (((1,), (0,)), ((), ())),
        preferred_element_type=jnp.float32,
    )
    rank = jnp.where(named > 0, rank, -1.0).astype(jnp.int32)
    slot = lax.broadcasted_iota(jnp.int32, (CAP, tokens), 0)
    grads = grads_ref[...]
    for e in range(experts):
        hit = rank[e : e + 1, :] == slot
        weight = jnp.sum(jnp.where(hit, gate[e : e + 1, :], 0.0), axis=1, keepdims=True)
        chosen = jnp.where(hit, 1.0, 0.0).astype(jnp.bfloat16)
        picked = lax.dot_general(
            chosen, grads, (((1,), (0,)), ((), ())), preferred_element_type=jnp.float32
        )
        out_ref[e] = (picked * weight).astype(out_ref.dtype)


def one_way_pair(array, axis, up, down, count):
    half = count // 2
    below, above = array, array
    pieces = []
    for step in range(1, half + 1):
        below = lax.ppermute(below, axis, up)
        pieces.append((-step, below))
        if step < half:
            above = lax.ppermute(above, axis, down)
            pieces.append((step, above))
    return pieces


def assemble_body(offsets, count, where_ref, *refs):
    piece_refs, out_ref = refs[:-1], refs[-1]
    me = where_ref[0]
    for offset, ref in zip(offsets, piece_refs):
        row = ((me + offset) % count) * CAP
        for i in range(ref.shape[0]):
            start = pl.multiple_of(i * count * CAP + row, CAP)
            out_ref[pl.ds(start, CAP), :] = ref[i]


def matmul_body(where_ref, mine_ref, other_ref, hidden_ref, out_ref):
    width = mine_ref.shape[1]
    core = where_ref[0]
    hidden = hidden_ref[...]
    for k, ref in enumerate((mine_ref, other_ref)):
        total = lax.dot_general(
            hidden, ref[...], (((0,), (0,)), ((), ())), preferred_element_type=jnp.float32
        )
        column = pl.multiple_of((core if k == 0 else 1 - core) * width, 128)
        out_ref[:, pl.ds(column, width)] = total.astype(out_ref.dtype)


def whole(array):
    return pl.BlockSpec(array.shape, lambda *_: (0,) * array.ndim)


def in_vmem(array):
    return pltpu.with_memory_space_constraint(array, pltpu.VMEM)


def local(grad_out, expert_ids, route_gates, saved_hidden):
    data_count = lax.axis_size("dp")
    expert_count = lax.axis_size("expert")
    tensor_count = lax.axis_size("tensor")
    chips = tensor_count // CORES
    width = grad_out.shape[1]
    x_up = [(k, (k + CORES) % tensor_count) for k in range(tensor_count)]
    x_down = [(k, (k - CORES) % tensor_count) for k in range(tensor_count)]
    swap = [(k, k ^ 1) for k in range(tensor_count)]
    same_core = [[c + CORES * k for k in range(chips)] for c in range(CORES)]

    hidden = lax.all_gather(saved_hidden[0], "dp", axis=0, tiled=True)

    slots = pl.pallas_call(
        lambda *refs: select_body(expert_count, *refs),
        out_shape=pltpu.VMEM((expert_count, CAP, width), jnp.bfloat16),
        name="select",
    )(expert_ids.T, route_gates.T, grad_out)
    slots = lax.all_to_all(slots, "expert", 0, 0, tiled=True)
    slots = lax.all_to_all(slots, "tensor", 0, 0, tiled=True, axis_index_groups=same_core)
    slots = lax.all_to_all(slots, "dp", 0, 0, tiled=True)
    pieces = [(0, slots), *one_way_pair(slots, "tensor", x_up, x_down, chips)]

    t = lax.axis_index("tensor")
    smem = pl.BlockSpec(memory_space=pltpu.SMEM)
    vmem = pl.BlockSpec(memory_space=pltpu.VMEM)
    mine = pl.pallas_call(
        lambda *refs: assemble_body([p[0] for p in pieces], chips, *refs),
        out_shape=pltpu.VMEM((data_count * chips * CAP, width), jnp.bfloat16),
        in_specs=[smem] + [vmem] * len(pieces),
        out_specs=vmem,
        name="assemble",
    )((t // CORES).astype(jnp.int32)[None], *[in_vmem(p[1]) for p in pieces])
    other = lax.ppermute(mine, "tensor", swap)

    rows, units = hidden.shape
    block = 256
    out = pl.pallas_call(
        matmul_body,
        out_shape=jax.ShapeDtypeStruct((units, CORES * width), jnp.bfloat16),
        grid=(units // block,),
        in_specs=[smem, vmem, vmem, pl.BlockSpec((rows, block), lambda g: (0, g))],
        out_specs=pl.BlockSpec((block, CORES * width), lambda g: (g, 0)),
        name="matmul",
    )((t % CORES).astype(jnp.int32)[None], in_vmem(mine), in_vmem(other), hidden)
    return out[None]


def solution(mesh):
    in_specs = (
        P(("dp", "expert"), "tensor"),
        P(("dp", "expert"), None),
        P(("dp", "expert"), None),
        P("expert", "dp", "tensor"),
    )
    out_specs = P("expert", "tensor", "dp")
    return jax.shard_map(local, mesh=mesh, in_specs=in_specs, out_specs=out_specs, check_vma=False)
```

time: 191 us -> 134 us (0.70)
  the two profiles are of different devices: /device:TPU:22 before, /device:TPU:1 now
where the time goes in v2:
time: 134 us; the launch traced here: 133 us
  blocking collectives  58.9 us (44%)
  starting transfers between devices  32.3 us (24%)
  waiting for transfers between devices  14.5 us (11%)
  between operations  13.5 us (10%)
  Pallas kernels  8.77 us (7%)
  local copies, waits for them, and re-layouts  5.14 us (4%)
    all_to_all x1, blocking collectives, local(): slots = lax.all_to_all(slots, 'expert', 0, 0, tiled=True)  26 us
    all_to_all x1, blocking collectives, local(): slots = lax.all_to_all(slots, 'dp', 0, 0, tiled=True)  17.9 us
    all_to_all x1, blocking collectives, local(): lax.all_to_all(slots, 'tensor', 0, 0, tiled=True, axis_index_groups=same_...  15 us
    ppermute x3, starting transfers between devices, one_way_pair(): above = lax.ppermute(above, axis, down)  13.6 us
    ppermute x4, waiting for transfers between devices, one_way_pair(): below = lax.ppermute(below, axis, up)  11.9 us
    ppermute x1, starting transfers between devices, local(): other = lax.ppermute(mine, 'tensor', swap)  10.9 us
    ppermute x4, starting transfers between devices, one_way_pair(): below = lax.ppermute(below, axis, up)  7.76 us
    pallas_call x1, Pallas kernels, local(): pl.pallas_call(matmul_body, out_shape=jax.ShapeDtypeStruct((units, CORES...  7.26 us
  transfers between devices with their start and end apart: 9, of which 5 were waited for; matrix products, arithmetic and copies ran while one was open for 0% of the time, Pallas kernels for 1%

profile of v2, /device:TPU:1, one launch (start us, length us, event | category | flops | bytes accessed | tf_op | source)
XLA Modules:
  0.0 133.1 jit_solution(14535339026965692942)
XLA Ops:
  6.5 0.7 all-gather.3.cloned.1.call-update
  7.3 1.3 select.7
  8.6 26.0 %all_to_all.15 = bf16[8,32,384]{2,1,0:T(8,128)(2,1)S(1)} all-to-all(bf16[8,32,384]{2,1,0:T(8,128)(2,1)S(1)} %select.7), channel_id=1, replica_groups=mesh['dp'=8,'expert'=8,'tensor'=16] {'expert'}, dimensions={0} | all-to-all | bytes 393216 | tf_op jit(solution)/shard_map/all_to_all | solution.py:105
  34.6 15.0 %all_to_all.16 = bf16[8,32,384]{2,1,0:T(8,128)(2,1)S(1)} all-to-all(bf16[8,32,384]{2,1,0:T(8,128)(2,1)S(1)} %all_to_all.15), channel_id=1, replica_groups={{0,2,4,6,8,10,12,14},{1,3,5,7,9,11,13,15},{16,18,20,22,24,26,28,30},{17..., dimensions={0} | all-to-all | bytes 393216 | tf_op jit(solution)/shard_map/all_to_all | solution.py:106
  49.6 17.9 %all_to_all.17.refs_1_ = bf16[8,32,384]{2,1,0:T(8,128)(2,1)S(1)} all-to-all(bf16[8,32,384]{2,1,0:T(8,128)(2,1)S(1)} %all_to_all.16), channel_id=1, replica_groups=mesh['dp'=8,'expert'=8,'tensor'=16] {'dp'}, dimensions={0} | all-to-all | bytes 393216 | tf_op jit(solution)/shard_map/all_to_all | solution.py:107
  67.5 2.0 %collective-permute-start = (bf16[8,32,384]{2,1,0:T(8,128)(2,1)S(1)}, bf16[8,32,384]{2,1,0:T(8,128)(2,1)S(1)}, u32[]{:S(2)}, u32[]{:S(2)}) collective-permute-start(bf16[8,32,384]{2,1,0:T(8,128)(2,1)S(1)} %all_to_all.17.refs_1_), channel_id=1, source_target_pairs={{0,2},{1,3},{2,4},{3,5},{4,6},{5,7},{6,8},{7,9},{8,10},{9,11},{10,... | collective-permute-start | bytes 589832 | tf_op jit(solution)/shard_map/ppermute | solution.py:49
  69.5 4.4 %collective-permute-start.1 = (bf16[8,32,384]{2,1,0:T(8,128)(2,1)S(1)}, bf16[8,32,384]{2,1,0:T(8,128)(2,1)S(1)}, u32[]{:S(2)}, u32[]{:S(2)}) collective-permute-start(bf16[8,32,384]{2,1,0:T(8,128)(2,1)S(1)} %all_to_all.17.refs_1_), channel_id=1, source_target_pairs={{0,14},{1,15},{2,0},{3,1},{4,2},{5,3},{6,4},{7,5},{8,6},{9,7},{10,... | collective-permute-start | bytes 589832 | tf_op jit(solution)/shard_map/ppermute | solution.py:52
  74.0 1.5 %collective-permute-done.refs_2_ = bf16[8,32,384]{2,1,0:T(8,128)(2,1)S(1)} collective-permute-done((bf16[8,32,384]{2,1,0:T(8,128)(2,1)S(1)}, bf16[8,32,384]{2,1,0:T(8,128)(2,1)S(1)}, u32[]{:S(2)}, u32[]{:S(2)}) %collective-permute-start) | collective-permute-done | bytes 196640 | tf_op jit(solution)/shard_map/ppermute | solution.py:49
  75.5 1.9 %collective-permute-start.2 = (bf16[8,32,384]{2,1,0:T(8,128)(2,1)S(1)}, bf16[8,32,384]{2,1,0:T(8,128)(2,1)S(1)}, u32[]{:S(2)}, u32[]{:S(2)}) collective-permute-start(bf16[8,32,384]{2,1,0:T(8,128)(2,1)S(1)} %collective-permute-done.refs_2_), channel_id=1, source_target_pairs={{0,2},{1,3},{2,4},{3,5},{4,6},{5,7},{6,8},{7,9},{8,10},{9,11},{10,... | collective-permute-start | bytes 589832 | tf_op jit(solution)/shard_map/ppermute | solution.py:49
  77.4 4.6 %collective-permute-start.3 = (bf16[8,32,384]{2,1,0:T(8,128)(2,1)S(1)}, bf16[8,32,384]{2,1,0:T(8,128)(2,1)S(1)}, u32[]{:S(2)}, u32[]{:S(2)}) collective-permute-start(bf16[8,32,384]{2,1,0:T(8,128)(2,1)S(1)} %collective-permute-done.1.refs_3_), channel_id=1, source_target_pairs={{0,14},{1,15},{2,0},{3,1},{4,2},{5,3},{6,4},{7,5},{8,6},{9,7},{10,... | collective-permute-start | bytes 589832 | tf_op jit(solution)/shard_map/ppermute | solution.py:52
  82.0 1.5 %collective-permute-done.2.refs_4_ = bf16[8,32,384]{2,1,0:T(8,128)(2,1)S(1)} collective-permute-done((bf16[8,32,384]{2,1,0:T(8,128)(2,1)S(1)}, bf16[8,32,384]{2,1,0:T(8,128)(2,1)S(1)}, u32[]{:S(2)}, u32[]{:S(2)}) %collective-permute-start.2) | collective-permute-done | bytes 196640 | tf_op jit(solution)/shard_map/ppermute | solution.py:49
  83.5 1.9 %collective-permute-start.4 = (bf16[8,32,384]{2,1,0:T(8,128)(2,1)S(1)}, bf16[8,32,384]{2,1,0:T(8,128)(2,1)S(1)}, u32[]{:S(2)}, u32[]{:S(2)}) collective-permute-start(bf16[8,32,384]{2,1,0:T(8,128)(2,1)S(1)} %collective-permute-done.2.refs_4_), channel_id=1, source_target_pairs={{0,2},{1,3},{2,4},{3,5},{4,6},{5,7},{6,8},{7,9},{8,10},{9,11},{10,... | collective-permute-start | bytes 589832 | tf_op jit(solution)/shard_map/ppermute | solution.py:49
  85.5 4.6 %collective-permute-start.5 = (bf16[8,32,384]{2,1,0:T(8,128)(2,1)S(1)}, bf16[8,32,384]{2,1,0:T(8,128)(2,1)S(1)}, u32[]{:S(2)}, u32[]{:S(2)}) collective-permute-start(bf16[8,32,384]{2,1,0:T(8,128)(2,1)S(1)} %collective-permute-done.3.refs_5_), channel_id=1, source_target_pairs={{0,14},{1,15},{2,0},{3,1},{4,2},{5,3},{6,4},{7,5},{8,6},{9,7},{10,... | collective-permute-start | bytes 589832 | tf_op jit(solution)/shard_map/ppermute | solution.py:52
  90.0 1.6 %collective-permute-done.4.refs_6_ = bf16[8,32,384]{2,1,0:T(8,128)(2,1)S(1)} collective-permute-done((bf16[8,32,384]{2,1,0:T(8,128)(2,1)S(1)}, bf16[8,32,384]{2,1,0:T(8,128)(2,1)S(1)}, u32[]{:S(2)}, u32[]{:S(2)}) %collective-permute-start.4) | collective-permute-done | bytes 196640 | tf_op jit(solution)/shard_map/ppermute | solution.py:49
  91.6 1.9 %collective-permute-start.6 = (bf16[8,32,384]{2,1,0:T(8,128)(2,1)S(1)}, bf16[8,32,384]{2,1,0:T(8,128)(2,1)S(1)}, u32[]{:S(2)}, u32[]{:S(2)}) collective-permute-start(bf16[8,32,384]{2,1,0:T(8,128)(2,1)S(1)} %collective-permute-done.4.refs_6_), channel_id=1, source_target_pairs={{0,2},{1,3},{2,4},{3,5},{4,6},{5,7},{6,8},{7,9},{8,10},{9,11},{10,... | collective-permute-start | bytes 589832 | tf_op jit(solution)/shard_map/ppermute | solution.py:49
  93.6 7.3 %collective-permute-done.6.refs_8_ = bf16[8,32,384]{2,1,0:T(8,128)(2,1)S(1)} collective-permute-done((bf16[8,32,384]{2,1,0:T(8,128)(2,1)S(1)}, bf16[8,32,384]{2,1,0:T(8,128)(2,1)S(1)}, u32[]{:S(2)}, u32[]{:S(2)}) %collective-permute-start.6) | collective-permute-done | bytes 196640 | tf_op jit(solution)/shard_map/ppermute | solution.py:49
  100.9 0.2 assemble.1.mine_ref
  101.1 10.9 %collective-permute-start.7 = (bf16[2048,384]{1,0:T(8,128)(2,1)S(1)}, bf16[2048,384]{1,0:T(8,128)(2,1)S(1)}, u32[]{:S(2)}, u32[]{:S(2)}) collective-permute-start(bf16[2048,384]{1,0:T(8,128)(2,1)S(1)} %assemble.1.mine_ref), channel_id=1, source_target_pairs={{0,1},{1,0},{2,3},{3,2},{4,5},{5,4},{6,7},{7,6},{8,9},{9,8},{10,11... | collective-permute-start | bytes 4718600 | tf_op jit(solution)/shard_map/ppermute | solution.py:120
  112.0 1.1 copy-done
  113.2 1.9 %collective-permute-done.7.other_ref = bf16[2048,384]{1,0:T(8,128)(2,1)S(1)} collective-permute-done((bf16[2048,384]{1,0:T(8,128)(2,1)S(1)}, bf16[2048,384]{1,0:T(8,128)(2,1)S(1)}, u32[]{:S(2)}, u32[]{:S(2)}) %collective-permute-start.7) | collective-permute-done | bytes 1572896 | tf_op jit(solution)/shard_map/ppermute | solution.py:120
  115.0 1.2 copy-done.2
  116.2 1.4 %copy-done.1 = bf16[2048,384]{1,0:T(8,128)(2,1)S(1)} copy-done((bf16[2048,384]{1,0:T(8,128)(2,1)S(1)}, bf16[2048,384]{1,0:T(8,128)(2,1)}, u32[]{:S(2)}) %copy-start.1) | copy-done | bytes 1572888
  117.6 1.4 %copy-done.3 = bf16[2048,384]{1,0:T(8,128)(2,1)S(1)} copy-done((bf16[2048,384]{1,0:T(8,128)(2,1)S(1)}, bf16[2048,384]{1,0:T(8,128)(2,1)}, u32[]{:S(2)}) %copy-start.3) | copy-done | bytes 1572888
  119.0 7.3 %matmul.1 = bf16[1024,768]{1,0:T(8,128)(2,1)} custom-call(s32[1]{0:T(128)} %bitcast.where_ref, bf16[2048,384]{1,0:T(8,128)(2,1)S(1)} %copy-done.1, bf16[2048,384]{1,0:T(8,128)(2,1)S(1)} %copy-done.3, bf16[2048,1024]{1,0:T(8,128)(2,1)} %bitcast.6), custom_call_target="tpu_custom_call" | custom-call | tf_op jit(solution)/shard_map/matmul/pallas_call | solution.py:124
  (9 shorter events, 0.0 us)
Async XLA Ops:
  6.5 109.7 %all-gather.3.cloned.1.call-start = ((), (), s32[]{:S(2)}) async-start(), calls=%async_computation.3 | async-start | bytes 4718592 | tf_op jit(solution)/shard_map/all_gather | solution.py:98
  67.5 8.0 %collective-permute-start = (bf16[8,32,384]{2,1,0:T(8,128)(2,1)S(1)}, bf16[8,32,384]{2,1,0:T(8,128)(2,1)S(1)}, u32[]{:S(2)}, u32[]{:S(2)}) collective-permute-start(bf16[8,32,384]{2,1,0:T(8,128)(2,1)S(1)} %all_to_all.17.refs_1_), channel_id=1, source_target_pairs={{0,2},{1,3},{2,4},{3,5},{4,6},{5,7},{6,8},{7,9},{8,10},{9,11},{10,... | collective-permute-start | bytes 589832 | tf_op jit(solution)/shard_map/ppermute | solution.py:49
  69.5 7.9 %collective-permute-start.1 = (bf16[8,32,384]{2,1,0:T(8,128)(2,1)S(1)}, bf16[8,32,384]{2,1,0:T(8,128)(2,1)S(1)}, u32[]{:S(2)}, u32[]{:S(2)}) collective-permute-start(bf16[8,32,384]{2,1,0:T(8,128)(2,1)S(1)} %all_to_all.17.refs_1_), channel_id=1, source_target_pairs={{0,14},{1,15},{2,0},{3,1},{4,2},{5,3},{6,4},{7,5},{8,6},{9,7},{10,... | collective-permute-start | bytes 589832 | tf_op jit(solution)/shard_map/ppermute | solution.py:52
  75.5 8.0 %collective-permute-start.2 = (bf16[8,32,384]{2,1,0:T(8,128)(2,1)S(1)}, bf16[8,32,384]{2,1,0:T(8,128)(2,1)S(1)}, u32[]{:S(2)}, u32[]{:S(2)}) collective-permute-start(bf16[8,32,384]{2,1,0:T(8,128)(2,1)S(1)} %collective-permute-done.refs_2_), channel_id=1, source_target_pairs={{0,2},{1,3},{2,4},{3,5},{4,6},{5,7},{6,8},{7,9},{8,10},{9,11},{10,... | collective-permute-start | bytes 589832 | tf_op jit(solution)/shard_map/ppermute | solution.py:49
  77.4 8.0 %collective-permute-start.3 = (bf16[8,32,384]{2,1,0:T(8,128)(2,1)S(1)}, bf16[8,32,384]{2,1,0:T(8,128)(2,1)S(1)}, u32[]{:S(2)}, u32[]{:S(2)}) collective-permute-start(bf16[8,32,384]{2,1,0:T(8,128)(2,1)S(1)} %collective-permute-done.1.refs_3_), channel_id=1, source_target_pairs={{0,14},{1,15},{2,0},{3,1},{4,2},{5,3},{6,4},{7,5},{8,6},{9,7},{10,... | collective-permute-start | bytes 589832 | tf_op jit(solution)/shard_map/ppermute | solution.py:52
  83.5 8.1 %collective-permute-start.4 = (bf16[8,32,384]{2,1,0:T(8,128)(2,1)S(1)}, bf16[8,32,384]{2,1,0:T(8,128)(2,1)S(1)}, u32[]{:S(2)}, u32[]{:S(2)}) collective-permute-start(bf16[8,32,384]{2,1,0:T(8,128)(2,1)S(1)} %collective-permute-done.2.refs_4_), channel_id=1, source_target_pairs={{0,2},{1,3},{2,4},{3,5},{4,6},{5,7},{6,8},{7,9},{8,10},{9,11},{10,... | collective-permute-start | bytes 589832 | tf_op jit(solution)/shard_map/ppermute | solution.py:49
  85.5 8.1 %collective-permute-start.5 = (bf16[8,32,384]{2,1,0:T(8,128)(2,1)S(1)}, bf16[8,32,384]{2,1,0:T(8,128)(2,1)S(1)}, u32[]{:S(2)}, u32[]{:S(2)}) collective-permute-start(bf16[8,32,384]{2,1,0:T(8,128)(2,1)S(1)} %collective-permute-done.3.refs_5_), channel_id=1, source_target_pairs={{0,14},{1,15},{2,0},{3,1},{4,2},{5,3},{6,4},{7,5},{8,6},{9,7},{10,... | collective-permute-start | bytes 589832 | tf_op jit(solution)/shard_map/ppermute | solution.py:52
  91.6 9.3 %collective-permute-start.6 = (bf16[8,32,384]{2,1,0:T(8,128)(2,1)S(1)}, bf16[8,32,384]{2,1,0:T(8,128)(2,1)S(1)}, u32[]{:S(2)}, u32[]{:S(2)}) collective-permute-start(bf16[8,32,384]{2,1,0:T(8,128)(2,1)S(1)} %collective-permute-done.4.refs_6_), channel_id=1, source_target_pairs={{0,2},{1,3},{2,4},{3,5},{4,6},{5,7},{6,8},{7,9},{8,10},{9,11},{10,... | collective-permute-start | bytes 589832 | tf_op jit(solution)/shard_map/ppermute | solution.py:49
  101.1 13.9 %collective-permute-start.7 = (bf16[2048,384]{1,0:T(8,128)(2,1)S(1)}, bf16[2048,384]{1,0:T(8,128)(2,1)S(1)}, u32[]{:S(2)}, u32[]{:S(2)}) collective-permute-start(bf16[2048,384]{1,0:T(8,128)(2,1)S(1)} %assemble.1.mine_ref), channel_id=1, source_target_pairs={{0,1},{1,0},{2,3},{3,2},{4,5},{5,4},{6,7},{7,6},{8,9},{9,8},{10,11... | collective-permute-start | bytes 4718600 | tf_op jit(solution)/shard_map/ppermute | solution.py:120
  112.0 1.1 copy-start
  115.0 1.2 copy-start.2
  116.2 1.4 %copy-start.1 = (bf16[2048,384]{1,0:T(8,128)(2,1)S(1)}, bf16[2048,384]{1,0:T(8,128)(2,1)}, u32[]{:S(2)}) copy-start(bf16[2048,384]{1,0:T(8,128)(2,1)} %copy-done) | copy-start | bytes 4718596
  117.6 1.4 %copy-start.3 = (bf16[2048,384]{1,0:T(8,128)(2,1)S(1)}, bf16[2048,384]{1,0:T(8,128)(2,1)}, u32[]{:S(2)}) copy-start(bf16[2048,384]{1,0:T(8,128)(2,1)} %copy-done.2) | copy-start | bytes 4718596
Sparse Core Ops, SparseCore 0:
  10.0 76.0 all-gather.2
